TPU v7x, 32 devices: a whole 2x2x4 slice. The times are simulated.
32 devices in a mesh: ctx: 16 (over z, y, core), head: 2 (over x).
Axes of the slice: x: 2, y: 2, z: 4, core: 2. Of those that a mesh axis runs over, the one named last changes fastest.
Arguments:
- hidden: bfloat16 [2048, 8192], P('ctx', 'head'), may hold values from -6 to 6
- query: bfloat16 [2048, 8192], P('ctx', 'head'), may hold values from -60 to 60
- fresh_key_value: bfloat16 [2, 2048, 1024], P(None, 'ctx', 'head'), may hold values from -6 to 6
- cached_key_value: bfloat16 [2, 4096, 1024], P(None, 'ctx', 'head'), may hold values from -6 to 6
- positions: int32 [3, 2048], P(None, 'ctx'), may hold values from 0 to 4095
- out_weight: bfloat16 [8192, 8192], P('head', 'ctx'), may hold values from -0.0625 to 0.0625
- norm_gain: float32 [8192], P('head'), may hold values from 0.25 to 1.75
- layer3_key_value_weight: bfloat16 [8192, 2048], P(None, 'head'), may hold values from -0.0625 to 0.0625
- layer3_key_value_bias: float32 [2048], P('head'), may hold values from -3 to 3
- keep_index: int32 [2048], P('ctx'), may hold values from 0 to 127, as said below
- keep_count: int32 [16], P('ctx'), may hold values from 64 to 128, as said below
Outputs:
- layer2_out: bfloat16 [2048, 8192], P('ctx', 'head')
- layer3_packed_key_value: bfloat16 [2048, 2048], P('ctx', 'head')
Inputs may be any that keep to these rules, and one draw needn't show every extreme that they name: `keep_index`: within each block of 128 entries, the first keep_count entries are the kept rows in rising order (all text rows and every second visual row), the rest the dropped rows in rising order. `keep_count`: some block keeps all 128 rows in every draw.
All inputs are finite; a program needn't handle non-finite values.
Results may differ from a plain program's by a relative error of at most 0.012.
Values may be sent and summed in bfloat16 or wider, within the bound.
A program may use at most 192 MiB of HBM per device.

v0:
```python
import jax
import jax.numpy as jnp
from jax import lax
from jax.sharding import PartitionSpec as P

MODEL_WIDTH = 8192
HEAD_DIMENSION = 128


def tables(positions, head_size):
    half = head_size // 2
    column = jnp.arange(half)
    frequency = jnp.power(jnp.float32(1000000.0), -(2.0 * column.astype(jnp.float32)) / head_size)
    section = (column >= head_size // 8).astype(jnp.int32) + (
        column >= head_size // 8 + 3 * head_size // 16
    ).astype(jnp.int32)
    places = positions.astype(jnp.float32)
    chosen = jnp.where(
        section[None, :] == 0,
        places[0][:, None],
        jnp.where(section[None, :] == 1, places[1][:, None], places[2][:, None]),
    )
    angles = chosen * frequency[None, :]
    return (jnp.cos(angles), jnp.sin(angles))


def apply_rotary(x, cosine_table, sine_table):
    half = x.shape[-1] // 2
    first_half = x[..., :half]
    second_half = x[..., half:]
    cosine_table = cosine_table[:, None, :]
    sine_table = sine_table[:, None, :]
    return jnp.concatenate(
        [
            first_half * cosine_table - second_half * sine_table,
            second_half * cosine_table + first_half * sine_table,
        ],
        axis=-1,
    )


def empty_state(rows, kv_local, query_group_width, head_size):
    return (
        jnp.full((rows, kv_local, query_group_width), -1e30, jnp.float32),
        jnp.zeros((rows, kv_local, query_group_width), jnp.float32),
        jnp.zeros((rows, kv_local, query_group_width, head_size), jnp.float32),
    )


def attend(grouped_rows, running, key_matrix_rows, value_matrix_rows, visible):
    head_size = grouped_rows.shape[-1]
    kv_local = grouped_rows.shape[1]
    key_heads = key_matrix_rows.reshape(key_matrix_rows.shape[0], kv_local, head_size)
    value_heads = value_matrix_rows.reshape(value_matrix_rows.shape[0], kv_local, head_size)
    scores = jnp.einsum(
        "nkgd,rkd->nkgr", grouped_rows, key_heads, preferred_element_type=jnp.float32
    ) * head_size ** (-0.5)
    if visible is not None:
        scores = jnp.where(visible[:, None, None, :], scores, -1e30)
    maxima, totals, weighted = running
    raised = jnp.maximum(maxima, jnp.max(scores, axis=-1))
    expos = jnp.exp(scores - raised[..., None])
    if visible is not None:
        expos = jnp.where(visible[:, None, None, :], expos, 0.0)
    factor = jnp.exp(maxima - raised)
    totals = totals * factor + jnp.sum(expos, axis=-1)
    weighted = weighted * factor[..., None] + jnp.einsum(
        "nkgr,rkd->nkgd",
        expos.astype(jnp.bfloat16),
        value_heads,
        preferred_element_type=jnp.float32,
    )
    return (raised, totals, weighted)


def local(
    hidden,
    query,
    fresh_key_value,
    cached_key_value,
    positions,
    out_weight,
    norm_gain,
    layer3_key_value_weight,
    layer3_key_value_bias,
    keep_index,
    keep_count,
):
    new_rows = hidden.shape[0]
    head_size = HEAD_DIMENSION
    kv_local = fresh_key_value.shape[2] // head_size
    q_local = query.shape[1] // head_size
    query_group_width = q_local // kv_local
    cosine_table, sine_table = tables(positions, head_size)
    rotary_query_rows = apply_rotary(
        query.astype(jnp.float32).reshape(new_rows, q_local, head_size), cosine_table, sine_table
    ).astype(jnp.bfloat16)
    grouped_rows = rotary_query_rows.reshape(new_rows, kv_local, query_group_width, head_size)
    rotary_key_rows = apply_rotary(
        fresh_key_value[0].astype(jnp.float32).reshape(new_rows, kv_local, head_size),
        cosine_table,
        sine_table,
    ).astype(jnp.bfloat16)
    recent = jnp.stack(
        [rotary_key_rows.reshape(new_rows, kv_local * head_size), fresh_key_value[1]]
    )
    first_row = lax.axis_index("ctx") * new_rows
    shard_piece = lax.all_gather(cached_key_value, "ctx", axis=1, tiled=True)
    running = attend(
        grouped_rows,
        empty_state(new_rows, kv_local, query_group_width, head_size),
        shard_piece[0],
        shard_piece[1],
        None,
    )
    query_pos = first_row + jnp.arange(new_rows)
    shard_piece = lax.all_gather(recent, "ctx", axis=1, tiled=True)
    key_pos = jnp.arange(shard_piece.shape[1])
    visible = key_pos[None, :] <= query_pos[:, None]
    maxima, totals, weighted = attend(
        grouped_rows, running, shard_piece[0], shard_piece[1], visible
    )
    attn = (
        (weighted / totals[..., None]).reshape(new_rows, q_local * head_size).astype(jnp.bfloat16)
    )
    outputs = lax.all_gather(attn, "ctx", axis=0, tiled=True)
    product = jnp.dot(outputs, out_weight, preferred_element_type=jnp.float32)
    partial_sum = lax.all_to_all(
        product.astype(jnp.bfloat16), "ctx", split_axis=0, concat_axis=1, tiled=True
    ).astype(product.dtype)
    head_summed = lax.psum_scatter(
        partial_sum.astype(jnp.bfloat16), "head", scatter_dimension=1, tiled=True
    ).astype(jnp.float32)
    layer2_out = (hidden.astype(jnp.float32) + head_summed).astype(jnp.bfloat16)
    widened = layer2_out.astype(jnp.float32)
    squares = lax.psum(jnp.sum(widened * widened, axis=1), "head")
    normalized_rows = (
        widened * lax.rsqrt(squares / MODEL_WIDTH + 1e-06)[:, None] * norm_gain
    ).astype(jnp.bfloat16)
    full_rows = lax.all_gather(normalized_rows, "head", axis=1, tiled=True)
    layer_three_key_value = (
        jnp.dot(full_rows, layer3_key_value_weight, preferred_element_type=jnp.float32)
        + layer3_key_value_bias
    ).reshape(new_rows, kv_local, 2, head_size)
    layer_three_keys = apply_rotary(layer_three_key_value[:, :, 0], cosine_table, sine_table)
    layer_three_key_value = (
        jnp.stack([layer_three_keys, layer_three_key_value[:, :, 1]], axis=2)
        .reshape(new_rows, 2 * kv_local * head_size)
        .astype(jnp.bfloat16)
    )
    selected_rows = jnp.take(layer_three_key_value, keep_index, axis=0)
    block_occupied = jnp.arange(new_rows) < keep_count[0]
    layer3_packed_key_value = jnp.where(
        block_occupied[:, None], selected_rows, jnp.zeros_like(selected_rows)
    )
    return (layer2_out, layer3_packed_key_value)


def solution(mesh):
    placed = (
        P("ctx", "head"),
        P("ctx", "head"),
        P(None, "ctx", "head"),
        P(None, "ctx", "head"),
        P(None, "ctx"),
        P("head", "ctx"),
        P("head"),
        P(None, "head"),
        P("head"),
        P("ctx"),
        P("ctx"),
    )
    return jax.shard_map(
        local,
        mesh=mesh,
        in_specs=placed,
        out_specs=(P("ctx", "head"), P("ctx", "head")),
        check_vma=False,
    )
```

profile of v0, /device:TPU:28, one launch (start us, length us, event | category | flops | bytes accessed | tf_op | source)
XLA Modules:
  0.0 538.2 jit_solution(5371693229478540200)
XLA Ops:
  7.2 0.0 all-gather.7.cloned.1.call-start
  7.2 0.8 convert_element_type.94
  8.0 1.0 fusion.34
  9.0 0.1 copy.59
  9.1 0.1 copy.58
  9.3 0.2 fusion.22
  9.6 0.7 pad_maximum_fusion.1
  10.3 0.0 all-gather.5.cloned.1.call-start
  10.4 2.0 copy.36
  12.4 0.0 all-gather.9.cloned.1.call-start
  12.5 0.1 copy.35
  12.6 0.1 copy.33
  12.7 0.2 convert_bitcast_fusion
  12.9 0.4 copy.63
  13.3 0.7 fusion.33
  14.0 2.4 subtract_convert_fusion
  16.5 0.2 iota_compare_fusion
  16.7 44.7 %all-gather.7.cloned.1.call-done = bf16[2,2048,512]{1,2,0:T(8,128)(2,1)} async-done(((bf16[2,128,512]{1,2,0:T(8,128)(2,1)}), bf16[2,2048,512]{1,2,0:T(8,128)(2,1)}) %all-gather.7.cloned.1.call-update) | async-done | bytes 4194320 | tf_op jit(solution)/shard_map/all_gather | solution.py:117
  61.3 4.1 fusion.32
  65.5 14.5 %fusion.5 = (f32[128,4,8]{0,2,1:T(8,128)S(1)}, f32[4,2048,128,8]{2,1,3,0:T(8,128)}) fusion(pred[128,2048]{0,1:T(8,128)(4,1)S(1)} %iota_compare_fusion, bf16[2048,4,128,1]{0,2,3,1:T(8,128)(2,1)S(1)} %bitcast.94, bf16[128,4,8,64]{3,0,2,1:T(8,128)(2,1)S(1)} %bitcast.91, bf16[128,4,8,64]{3,0,2,1:T(8,128)(2,1)S(1)} %bitcast.89), kind=kOutput, calls=%fused_computation.9 | convolution fusion | flops 2174742528 | bytes 36978688 | tf_op jit(solution)/shard_map/nkgd,rkd->nkgr/dot_general | solution.py:55
  80.0 60.0 %all-gather.5.cloned.1.call-done = bf16[2,4096,512]{1,2,0:T(8,128)(2,1)} async-done(((bf16[2,256,512]{1,2,0:T(8,128)(2,1)}), bf16[2,4096,512]{1,2,0:T(8,128)(2,1)}) %all-gather.5.cloned.1.call-update) | async-done | bytes 8388624 | tf_op jit(solution)/shard_map/all_gather | solution.py:108
  140.0 6.0 %fusion.31 = (bf16[1,4096,512]{1,2,0:T(8,128)(2,1)}, bf16[1,4096,512]{1,2,0:T(8,128)(2,1)}) fusion(bf16[2,4096,512]{1,2,0:T(8,128)(2,1)} %all-gather.5.cloned.1.call-done), kind=kLoop, calls=%fused_computation.73 | loop fusion | bytes 16777216 | tf_op jit(solution)/shard_map/slice | solution.py:112
  146.0 25.7 %bitcast_reduce_fusion = (f32[128,4,8]{0,2,1:T(8,128)S(1)}, f32[4,128,8,4096]{3,1,2,0:T(8,128)}) fusion(bf16[4096,4,128,1]{0,2,3,1:T(8,128)(2,1)} %bitcast.88, bf16[128,4,8,64]{3,0,2,1:T(8,128)(2,1)S(1)} %bitcast.92, bf16[128,4,8,64]{3,0,2,1:T(8,128)(2,1)S(1)} %bitcast.90), kind=kOutput, calls=%fused_computation.2 | convolution fusion | flops 4330614784 | bytes 72368128 | tf_op jit(solution)/shard_map/nkgd,rkd->nkgr/dot_general | solution.py:55
  171.7 21.2 %fusion.1 = f32[128,4,8]{0,2,1:T(8,128)S(1)} fusion(f32[4,128,8,4096]{3,1,2,0:T(8,128)} %get-tuple-element.29, f32[128,4,8]{0,2,1:T(8,128)S(1)} %get-tuple-element.22), kind=kLoop, calls=%fused_computation.4 | loop fusion | flops 50327552 | bytes 67141632 | tf_op jit(solution)/shard_map/reduce_sum | solution.py:66
  193.0 25.2 %fusion.3 = f32[4,128,8,128]{1,3,2,0:T(8,128)S(1)} fusion(bf16[4096,4,128,1]{0,2,3,1:T(8,128)(2,1)} %bitcast.87, f32[4,128,8,4096]{3,1,2,0:T(8,128)} %get-tuple-element.29, f32[128,4,8]{0,2,1:T(8,128)S(1)} %get-tuple-element.22), kind=kOutput, calls=%fused_computation.8 | convolution fusion | flops 4345298944 | bytes 73416704 | tf_op jit(solution)/shard_map/nkgr,rkd->nkgd/dot_general | solution.py:67
  218.2 14.8 %fusion.6 = f32[128,4,8]{0,2,1:T(8,128)S(1)} fusion(f32[4,2048,128,8]{2,1,3,0:T(8,128)} %get-tuple-element.31, f32[128,4,8]{0,2,1:T(8,128)S(1)} %get-tuple-element.21, pred[128,2048]{0,1:T(8,128)(4,1)S(1)} %iota_compare_fusion), kind=kLoop, calls=%fused_computation.10 | loop fusion | flops 41938944 | bytes 33849344 | tf_op jit(solution)/shard_map/reduce_sum | solution.py:66
  233.0 16.3 %fusion.15 = bf16[128,4,8,128]{0,3,2,1:T(8,128)(2,1)} fusion(f32[4,128,8,128]{1,3,2,0:T(8,128)S(1)} %fusion.3, bf16[2048,4,128,1]{0,2,3,1:T(8,128)(2,1)} %bitcast.97, f32[4,2048,128,8]{2,1,3,0:T(8,128)} %get-tuple-element.31, f32[128,4,8]{0,2,1:T(8,128)S(1)} %get-tuple-element.21, pred[128,2048]{0,1:T(8,128)(4,1)S(1)} %iota_compare_fusion, ...), kind=kOutput, calls=%fused_computation.22 | convolution fusion | flops 2192048128 | bytes 39124992 | tf_op jit(solution)/shard_map/nkgr,rkd->nkgd/dot_general | solution.py:67
  249.4 0.0 reduce-scatter.2.cloned.1.call-start
  249.4 128.2 %all-gather.9.cloned.1.call-done = bf16[2048,4096]{0,1:T(8,128)(2,1)} async-done(((bf16[128,4096]{0,1:T(8,128)(2,1)}), bf16[2048,4096]{0,1:T(8,128)(2,1)}) %all-gather.9.cloned.1.call-update) | async-done | bytes 16777232 | tf_op jit(solution)/shard_map/all_gather | solution.py:126
  377.6 13.6 %convolution_convert_fusion = bf16[2048,512]{1,0:T(8,128)(2,1)S(1)} fusion(bf16[2048,4096]{0,1:T(8,128)(2,1)} %all-gather.9.cloned.1.call-done, bf16[4096,512]{1,0:T(8,128)(2,1)} %param.16), kind=kOutput, calls=%fused_computation.14 | convolution fusion | flops 8590983168 | bytes 23068672 | tf_op jit(solution)/shard_map/dot_general | solution.py:127
  391.2 52.2 %all_to_all.19 = bf16[16,128,512]{2,1,0:T(8,128)(2,1)S(1)} all-to-all(bf16[16,128,512]{2,1,0:T(8,128)(2,1)S(1)} %bitcast.96), channel_id=1, replica_groups=mesh['ctx'=16,'head'=2] {'ctx'}, dimensions={0} | all-to-all | bytes 4194304 | tf_op jit(solution)/shard_map/all_to_all | solution.py:128
  443.4 1.6 copy.62
  445.0 0.0 all-gather.11.cloned.1.call-start
  445.0 33.0 %reduce-scatter.2.cloned.1.call-done = bf16[128,4096]{1,0:T(8,128)(2,1)} async-done(((bf16[128,8192]{1,0:T(8,128)(2,1)}), bf16[128,4096]{1,0:T(8,128)(2,1)}) %reduce-scatter.2.cloned.1.call-update) | async-done | bytes 1048592 | tf_op jit(solution)/shard_map/reduce_scatter | solution.py:131
  478.0 1.7 fusion.11
  479.7 5.2 psum.7
  484.9 1.3 fusion.13
  486.9 32.5 %all-gather.11.cloned.1.call-done = bf16[128,8192]{1,0:T(8,128)(2,1)} async-done(((bf16[128,4096]{1,0:T(8,128)(2,1)}), bf16[128,8192]{1,0:T(8,128)(2,1)}) %all-gather.11.cloned.1.call-update) | async-done | bytes 2097168 | tf_op jit(solution)/shard_map/all_gather | solution.py:140
  519.5 8.7 %convolution_add_fusion = f32[128,1024]{1,0:T(8,128)S(1)} fusion(bf16[128,8192]{1,0:T(8,128)(2,1)} %all-gather.11.cloned.1.call-done, bf16[8192,1024]{1,0:T(8,128)(2,1)} %param.18, f32[1024]{0:T(1024)S(1)} %copy-done.4), kind=kOutput, calls=%fused_computation.29 | convolution fusion | flops 2147614720 | bytes 19402752 | tf_op jit(solution)/shard_map/dot_general | solution.py:142
  528.2 0.4 reshape.280
  528.7 0.3 slice.82
  529.0 0.2 slice.79
  529.2 0.1 copy.60
  529.4 0.1 copy.44
  529.6 0.3 copy.46
  529.8 0.2 convert_element_type.108
  530.0 0.9 gather_fusion
  530.9 0.8 select_select_fusion
  (34 shorter events, 0.4 us)
Async XLA Ops:
  7.2 5.5 %copy-start.1 = (bf16[128,4096]{1,0:T(8,128)(2,1)S(1)}, bf16[128,4096]{1,0:T(8,128)(2,1)}, u32[]{:S(2)}) copy-start(bf16[128,4096]{1,0:T(8,128)(2,1)} %param.12) | copy-start | bytes 3145732
  7.2 54.2 %all-gather.7.cloned.1.call-start = ((), (), s32[]{:S(2)}) async-start(), calls=%async_computation.3 | async-start | bytes 4456448 | tf_op jit(solution)/shard_map/all_gather | solution.py:117
  10.3 129.7 %all-gather.5.cloned.1.call-start = ((), (), s32[]{:S(2)}) async-start(), calls=%async_computation.2 | async-start | bytes 8912896 | tf_op jit(solution)/shard_map/all_gather | solution.py:108
  12.4 365.1 %all-gather.9.cloned.1.call-start = ((), (), s32[]{:S(2)}) async-start(), calls=%async_computation.4 | async-start | bytes 17825792 | tf_op jit(solution)/shard_map/all_gather | solution.py:126
  249.4 228.6 %reduce-scatter.2.cloned.1.call-start = ((), (), s32[]{:S(2)}) async-start(), calls=%async_computation.5 | async-start | bytes 3145728 | tf_op jit(solution)/shard_map/reduce_scatter | solution.py:131
  443.4 34.6 %copy-start.2 = (bf16[128,4096]{1,0:T(8,128)(2,1)S(1)}, bf16[128,4096]{1,0:T(8,128)(2,1)}, u32[]{:S(2)}) copy-start(bf16[128,4096]{1,0:T(8,128)(2,1)} %param.11) | copy-start | bytes 3145732
  443.4 41.5 %copy-start.3 = (f32[4096]{0:T(1024)S(1)}, f32[4096]{0:T(1024)}, u32[]{:S(2)}) copy-start(f32[4096]{0:T(1024)} %param.17) | copy-start | bytes 49156
  445.0 41.9 %copy-start.5 = (s32[128]{0:T(128)S(1)}, s32[128]{0:T(128)}, u32[]{:S(2)}) copy-start(s32[128]{0:T(128)} %param.20) | copy-start | bytes 1540
  445.0 74.5 %copy-start.4 = (f32[1024]{0:T(1024)S(1)}, f32[1024]{0:T(1024)}, u32[]{:S(2)}) copy-start(f32[1024]{0:T(1024)} %param.19) | copy-start | bytes 12292
  445.0 74.5 %all-gather.11.cloned.1.call-start = ((), (), s32[]{:S(2)}) async-start(), calls=%async_computation.6 | async-start | bytes 3145728 | tf_op jit(solution)/shard_map/all_gather | solution.py:140
  479.7 48.5 %copy-start = (bf16[128,4096]{1,0:T(8,128)(2,1)}, bf16[128,4096]{1,0:T(8,128)(2,1)S(1)}, u32[]{:S(2)}) copy-start(bf16[128,4096]{1,0:T(8,128)(2,1)S(1)} %get-tuple-element.3) | copy-start | bytes 3145732
Sparse Core Ops, SparseCore 0:
  10.7 50.5 all-gather.6
  64.1 75.8 all-gather.4
  249.5 128.0 all-gather.8
  445.1 32.8 reduce-scatter.1
  486.4 33.0 all-gather.10
where the time goes:
time: 541 us; the launch traced here: 538 us
  waiting for transfers between devices  298 us (55%)
  matrix products  104 us (19%)
  blocking collectives  57.4 us (11%)
  other arithmetic  44.6 us (8%)
  local copies, waits for them, and re-layouts  18.7 us (3%)
  between operations  14.7 us (3%)
    all_gather x1, waiting for transfers between devices, local(): outputs = lax.all_gather(attn, 'ctx', axis=0, tiled=True)  128 us
    all_gather x1, waiting for transfers between devices, local(): shard_piece = lax.all_gather(cached_key_value, 'ctx', axis=1, tiled=True)  60 us
    all_to_all x1, blocking collectives, local(): lax.all_to_all(product.astype(jnp.bfloat16), 'ctx', split_axis=0, concat_...  52.2 us
    all_gather x1, waiting for transfers between devices, local(): shard_piece = lax.all_gather(recent, 'ctx', axis=1, tiled=True)  44.7 us
    dot_general x2, matrix products, attend(): jnp.einsum('nkgr,rkd->nkgd', expos.astype(jnp.bfloat16), value_heads, pre...  41.5 us
    dot_general x2, matrix products, attend(): jnp.einsum('nkgd,rkd->nkgr', grouped_rows, key_heads, preferred_element_t...  40.2 us
    reduce_sum x2, other arithmetic, attend(): totals = totals * factor + jnp.sum(expos, axis=-1)  36.1 us
    reduce_scatter x1, waiting for transfers between devices, local(): lax.psum_scatter(partial_sum.astype(jnp.bfloat16), 'head', scatter_dimens...  33 us
  transfers between devices with their start and end apart: 5, of which 5 were waited for; matrix products, arithmetic and copies ran while one was open for 5% of the time, Pallas kernels for 0%

commit v1 on v0

v1 whole, which is shorter than its diff:
```python
import functools

import jax
import jax.numpy as jnp
from jax import lax
from jax.experimental import pallas as pl
from jax.experimental.pallas import tpu as pltpu
from jax.sharding import PartitionSpec as P

HEAD_DIMENSION = 128


def tables(positions, head_size):
    half = head_size // 2
    column = jnp.arange(half)
    frequency = jnp.power(jnp.float32(1000000.0), -(2.0 * column.astype(jnp.float32)) / head_size)
    section = (column >= head_size // 8).astype(jnp.int32) + (
        column >= head_size // 8 + 3 * head_size // 16
    ).astype(jnp.int32)
    places = positions.astype(jnp.float32)
    chosen = jnp.where(
        section[None, :] == 0,
        places[0][:, None],
        jnp.where(section[None, :] == 1, places[1][:, None], places[2][:, None]),
    )
    angles = chosen * frequency[None, :]
    return (jnp.cos(angles), jnp.sin(angles))


def apply_rotary(x, cosine_table, sine_table):
    half = x.shape[-1] // 2
    first_half = x[..., :half]
    second_half = x[..., half:]
    cosine_table = cosine_table[:, None, :]
    sine_table = sine_table[:, None, :]
    return jnp.concatenate(
        [
            first_half * cosine_table - second_half * sine_table,
            second_half * cosine_table + first_half * sine_table,
        ],
        axis=-1,
    )


LOG2E = 1.4426950408889634


def attend_kernel(group, causal, last, row_ref, q_ref, k_ref, v_ref, *rest):
    if last:
        m_in, l_in, a_in, out_ref, m_ref, l_ref, a_ref = rest
    else:
        m_out, l_out, a_out, m_ref, l_ref, a_ref = rest
    step = pl.program_id(1)
    head = k_ref.shape[1]
    rows = q_ref.shape[0]
    block = k_ref.shape[0]

    @pl.when(step == 0)
    def _():
        if last:
            m_ref[...] = m_in[0]
            l_ref[...] = l_in[0]
            a_ref[...] = a_in[0]
        else:
            m_ref[...] = jnp.full_like(m_ref, -1e30)
            l_ref[...] = jnp.zeros_like(l_ref)
            a_ref[...] = jnp.zeros_like(a_ref)

    def update(masked):
        key = k_ref[...]
        value = v_ref[...]
        scale = LOG2E * head ** (-0.5)
        if masked:
            key_pos = step * block + lax.broadcasted_iota(jnp.int32, (rows, block), 1)
            query_pos = row_ref[0] + lax.broadcasted_iota(jnp.int32, (rows, block), 0)
            visible = key_pos <= query_pos
        for g in range(group):
            part = pl.ds(g * rows, rows)
            s = lax.dot_general(
                q_ref[:, g * head : (g + 1) * head],
                key,
                (((1,), (1,)), ((), ())),
                preferred_element_type=jnp.float32,
            )
            if masked:
                s = jnp.where(visible, s, -1e30)
            old = m_ref[part, :]
            new = jnp.maximum(old, jnp.max(s, axis=1, keepdims=True))
            m_ref[part, :] = new
            e = jnp.exp2((s - new[:, :1]) * scale)
            factor = jnp.exp2((old - new) * scale)
            l_ref[part, :] = l_ref[part, :] * factor + jnp.sum(e, axis=1, keepdims=True)
            a_ref[part, :] = a_ref[part, :] * factor + jnp.dot(
                e.astype(jnp.bfloat16), value, preferred_element_type=jnp.float32
            )

    if causal:
        start = step * block

        @pl.when(start + block - 1 <= row_ref[0])
        def _():
            update(False)

        @pl.when((start + block - 1 > row_ref[0]) & (start <= row_ref[0] + rows - 1))
        def _():
            update(True)
    else:
        update(False)

    @pl.when(step == pl.num_programs(1) - 1)
    def _():
        if last:
            for g in range(group):
                part = pl.ds(g * rows, rows)
                out_ref[:, g * head : (g + 1) * head] = (
                    a_ref[part, :] / l_ref[part, :]
                ).astype(out_ref.dtype)
        else:
            m_out[0] = m_ref[...]
            l_out[0] = l_ref[...]
            a_out[0] = a_ref[...]


def attend(query, key_value, first_row, state, head_size):
    rows, width = query.shape
    length = key_value.shape[1]
    kv_local = key_value.shape[2] // head_size
    group = width // head_size // kv_local
    block = 1024
    while length % block:
        block //= 2
    last = state is not None
    high = group * rows
    carry = pl.BlockSpec((1, high, head_size), lambda k, i, r: (k, 0, 0))
    carry_shape = jax.ShapeDtypeStruct((kv_local, high, head_size), jnp.float32)
    wide = pl.BlockSpec((rows, group * head_size), lambda k, i, r: (0, k))
    in_specs = [
        wide,
        pl.BlockSpec((None, block, head_size), lambda k, i, r: (0, i, k)),
        pl.BlockSpec((None, block, head_size), lambda k, i, r: (1, i, k)),
    ] + ([carry] * 3 if last else [])
    operands = (query, key_value, key_value) + (state if last else ())
    return pl.pallas_call(
        functools.partial(attend_kernel, group, last, last),
        out_shape=jax.ShapeDtypeStruct((rows, width), jnp.bfloat16) if last else (carry_shape,) * 3,
        grid_spec=pltpu.PrefetchScalarGridSpec(
            num_scalar_prefetch=1,
            grid=(kv_local, length // block),
            in_specs=in_specs,
            out_specs=wide if last else (carry,) * 3,
            scratch_shapes=[pltpu.VMEM((high, head_size), jnp.float32)] * 3,
        ),
        compiler_params=pltpu.CompilerParams(vmem_limit_bytes=40 * 1024 * 1024),
        cost_estimate=pl.CostEstimate(
            flops=8 * rows * width * length,
            bytes_accessed=4 * length * kv_local * head_size + 4 * rows * width,
            transcendentals=rows * (width // head_size) * length,
        ),
    )(first_row.reshape(1), *operands)


def scatter_kernel(chips, cores, heads, x_ref, o_ref, send_sem, recv_sem, tile, local_sem):
    me = lax.axis_index("ctx")
    h = lax.axis_index("head")
    chip = me // cores
    core = me % cores
    per = chips // heads
    owner_head = chip // per
    slot = h * per + chip % per
    barrier = pltpu.get_barrier_semaphore()
    for d in range(chips):
        there = lax.rem(chip + d, chips) * cores + core
        for e in range(heads):
            if d or e:
                pl.semaphore_signal(
                    barrier,
                    inc=1,
                    device_id=(there, lax.rem(h + e, heads)),
                    device_id_type=pl.DeviceIdType.MESH,
                )
    pl.semaphore_wait(barrier, chips * heads - 1)

    def copy_to(d):
        p = lax.rem(chip + d, chips)
        return pltpu.make_async_remote_copy(
            src_ref=x_ref.at[p],
            dst_ref=o_ref.at[slot],
            send_sem=send_sem.at[d],
            recv_sem=recv_sem.at[slot],
            device_id=(p * cores + core, owner_head),
            device_id_type=pl.DeviceIdType.MESH,
        )

    def receive(s):
        return pltpu.make_async_remote_copy(
            src_ref=x_ref.at[0],
            dst_ref=o_ref.at[s],
            send_sem=send_sem.at[0],
            recv_sem=recv_sem.at[s],
            device_id=(me, lax.rem(h + 1, heads)),
            device_id_type=pl.DeviceIdType.MESH,
        )

    for d in range(1, chips):
        copy_to(d).start()

    @pl.when(owner_head != h)
    def _():
        copy_to(0).start()

    @pl.when(owner_head == h)
    def _():
        into = pltpu.make_async_copy(x_ref.at[chip], tile, local_sem.at[0])
        into.start()
        into.wait()
        out = pltpu.make_async_copy(tile, o_ref.at[slot], local_sem.at[1])
        out.start()
        out.wait()

    for d in range(1, chips):
        copy_to(d).wait_send()

    @pl.when(owner_head != h)
    def _():
        copy_to(0).wait_send()

    for s in range(chips):

        @pl.when(jnp.logical_or(owner_head != h, slot != s))
        def _():
            receive(s).wait_recv()


def scatter_columns(product, chips, cores, heads):
    block = product.shape[1:]
    moved = pl.pallas_call(
        functools.partial(scatter_kernel, chips, cores, heads),
        out_shape=jax.ShapeDtypeStruct(product.shape, product.dtype),
        in_specs=[pl.BlockSpec(memory_space=pl.ANY)],
        out_specs=pl.BlockSpec(memory_space=pl.ANY),
        scratch_shapes=[
            pltpu.SemaphoreType.DMA((chips,)),
            pltpu.SemaphoreType.DMA((chips,)),
            pltpu.VMEM(block, product.dtype),
            pltpu.SemaphoreType.DMA((2,)),
        ],
        compiler_params=pltpu.CompilerParams(collective_id=0, has_side_effects=True),
    )(product)
    return moved.reshape((heads, chips // heads) + block)


def gather_kernel(depth, cores, x_ref, o_ref, send_sem, recv_sem, tile, local_sem):
    me = lax.axis_index("ctx")
    h = lax.axis_index("head")
    chip = me // cores
    core = me % cores
    ring = chip // 2
    side = chip % 2
    pair = ring * 2 + (1 - side)

    def along(d):
        return lax.rem(ring + d, depth)

    barrier = pltpu.get_barrier_semaphore()
    for d in range(1, depth):
        pl.semaphore_signal(
            barrier,
            inc=1,
            device_id=((along(d) * 2 + side) * cores + core, h),
            device_id_type=pl.DeviceIdType.MESH,
        )
    pl.semaphore_signal(
        barrier, inc=1, device_id=(pair * cores + core, h), device_id_type=pl.DeviceIdType.MESH
    )
    pl.semaphore_wait(barrier, depth)

    def send(source, half, origin, target, kind, d):
        return pltpu.make_async_remote_copy(
            src_ref=source,
            dst_ref=o_ref.at[origin, half],
            send_sem=send_sem.at[kind, d],
            recv_sem=recv_sem.at[half, origin],
            device_id=(target * cores + core, h),
            device_id_type=pl.DeviceIdType.MESH,
        )

    def receive(half, origin):
        send(x_ref.at[half], half, origin, pair, 0, 0).wait_recv()

    sent = [send(x_ref.at[0], 0, chip, pair, 0, 0), send(x_ref.at[1], 1, chip, pair, 1, 0)]
    order = [d for pair_of in zip(range(1, depth), range(depth - 1, 0, -1)) for d in pair_of]
    order = list(dict.fromkeys(order))
    for d in order:
        sent.append(send(x_ref.at[1], 1, chip, along(d) * 2 + side, 2, d))
    for d in order:
        sent.append(send(x_ref.at[0], 0, chip, along(d) * 2 + side, 3, d))
    for copy in sent:
        copy.start()
    into = pltpu.make_async_copy(x_ref, tile, local_sem.at[0])
    into.start()
    into.wait()
    out = pltpu.make_async_copy(tile, o_ref.at[chip], local_sem.at[1])
    out.start()

    receive(0, pair)
    for d in order:
        copy = send(o_ref.at[pair, 0], 0, pair, along(d) * 2 + side, 4, d)
        copy.start()
        sent.append(copy)
    for d in order:
        origin = along(d) * 2 + side
        receive(1, origin)
        copy = send(o_ref.at[origin, 1], 1, origin, pair, 1, d)
        copy.start()
        sent.append(copy)
    for d in range(1, depth):
        receive(0, along(d) * 2 + side)
    receive(1, pair)
    for d in range(1, depth):
        receive(0, along(d) * 2 + 1 - side)
        receive(1, along(d) * 2 + 1 - side)
    for copy in sent:
        copy.wait_send()
    out.wait()


def gather_rows(x, chips, cores):
    rows, width = x.shape
    halves = x.reshape(2, rows // 2, width)
    return pl.pallas_call(
        functools.partial(gather_kernel, chips // 2, cores),
        out_shape=jax.ShapeDtypeStruct((chips,) + halves.shape, x.dtype),
        in_specs=[pl.BlockSpec(memory_space=pl.ANY)],
        out_specs=pl.BlockSpec(memory_space=pl.ANY),
        scratch_shapes=[
            pltpu.SemaphoreType.DMA((5, chips // 2)),
            pltpu.SemaphoreType.DMA((2, chips)),
            pltpu.VMEM(halves.shape, x.dtype),
            pltpu.SemaphoreType.DMA((2,)),
        ],
        compiler_params=pltpu.CompilerParams(collective_id=1, has_side_effects=True),
    )(halves).reshape(chips * rows, width)


def exchange(x, axis_name, size):
    return lax.ppermute(x, axis_name, [(i, i ^ 1) for i in range(size)])


def local(
    contexts,
    heads,
    hidden,
    query,
    fresh_key_value,
    cached_key_value,
    positions,
    out_weight,
    norm_gain,
    layer3_key_value_weight,
    layer3_key_value_bias,
    keep_index,
    keep_count,
):
    new_rows = hidden.shape[0]
    head_size = HEAD_DIMENSION
    kv_local = fresh_key_value.shape[2] // head_size
    q_local = query.shape[1] // head_size
    cores = 2
    chips = contexts // cores
    me = lax.axis_index("ctx")
    core = me % cores
    head = lax.axis_index("head")
    cosine_table, sine_table = tables(positions, head_size)
    rotary_query_rows = apply_rotary(
        query.astype(jnp.float32).reshape(new_rows, q_local, head_size), cosine_table, sine_table
    ).astype(jnp.bfloat16).reshape(new_rows, q_local * head_size)
    rotary_key_rows = apply_rotary(
        fresh_key_value[0].astype(jnp.float32).reshape(new_rows, kv_local, head_size),
        cosine_table,
        sine_table,
    ).astype(jnp.bfloat16)
    recent = jnp.stack(
        [rotary_key_rows.reshape(new_rows, kv_local * head_size), fresh_key_value[1]]
    )
    if heads == 2:
        other_gain = exchange(norm_gain, "head", heads)
        whole_gain = jnp.concatenate(
            [jnp.where(head == 0, norm_gain, other_gain), jnp.where(head == 0, other_gain, norm_gain)]
        )
    else:
        whole_gain = lax.all_gather(norm_gain, "head", axis=0, tiled=True)
    other_weight = exchange(out_weight, "ctx", contexts)
    first_row = me * new_rows
    cached_all = lax.all_gather(cached_key_value, "ctx", axis=1, tiled=True)
    recent_all = lax.all_gather(recent, "ctx", axis=1, tiled=True)
    state = attend(rotary_query_rows, cached_all, first_row, None, head_size)
    attn = attend(rotary_query_rows, recent_all, first_row, tuple(state), head_size)
    outputs = gather_rows(attn, chips, cores)
    own = jnp.dot(outputs, out_weight, preferred_element_type=jnp.float32).astype(jnp.bfloat16)
    other = jnp.dot(outputs, other_weight, preferred_element_type=jnp.float32).astype(jnp.bfloat16)
    product = jnp.concatenate(
        [jnp.where(core == 0, own, other), jnp.where(core == 0, other, own)], axis=1
    ).reshape(chips, new_rows, -1)
    parts = scatter_columns(product, chips, cores, heads)
    head_summed = jnp.sum(parts.astype(jnp.float32), axis=0)
    head_summed = head_summed.transpose(1, 0, 2).reshape(hidden.shape)
    layer2_out = (hidden.astype(jnp.float32) + head_summed).astype(jnp.bfloat16)
    if heads == 2:
        other_out = exchange(layer2_out, "head", heads)
        whole_out = jnp.concatenate(
            [
                jnp.where(head == 0, layer2_out, other_out),
                jnp.where(head == 0, other_out, layer2_out),
            ],
            axis=1,
        )
    else:
        whole_out = lax.all_gather(layer2_out, "head", axis=1, tiled=True)
    widened = whole_out.astype(jnp.float32)
    squares = jnp.sum(widened * widened, axis=1)
    level = lax.rsqrt(squares / widened.shape[1] + 1e-06)[:, None]
    full_rows = (widened * level * whole_gain).astype(jnp.bfloat16)
    full_rows = lax.optimization_barrier(full_rows)
    layer_three_key_value = (
        jnp.dot(full_rows, layer3_key_value_weight, preferred_element_type=jnp.float32)
        + layer3_key_value_bias
    ).reshape(new_rows, kv_local, 2, head_size)
    layer_three_keys = apply_rotary(layer_three_key_value[:, :, 0], cosine_table, sine_table)
    layer_three_key_value = (
        jnp.stack([layer_three_keys, layer_three_key_value[:, :, 1]], axis=2)
        .reshape(new_rows, 2 * kv_local * head_size)
        .astype(jnp.bfloat16)
    )
    selected_rows = jnp.take(layer_three_key_value, keep_index, axis=0)
    block_occupied = jnp.arange(new_rows) < keep_count[0]
    layer3_packed_key_value = jnp.where(
        block_occupied[:, None], selected_rows, jnp.zeros_like(selected_rows)
    )
    return (layer2_out, layer3_packed_key_value)


def solution(mesh):
    placed = (
        P("ctx", "head"),
        P("ctx", "head"),
        P(None, "ctx", "head"),
        P(None, "ctx", "head"),
        P(None, "ctx"),
        P("head", "ctx"),
        P("head"),
        P(None, "head"),
        P("head"),
        P("ctx"),
        P("ctx"),
    )
    return jax.shard_map(
        functools.partial(local, mesh.shape["ctx"], mesh.shape["head"]),
        mesh=mesh,
        in_specs=placed,
        out_specs=(P("ctx", "head"), P("ctx", "head")),
        check_vma=False,
    )
```

time: 541 us -> 463 us (0.86)
  Pallas kernels: 0 us -> 287 us
  waiting for transfers between devices: 298 us -> 90 us
  matrix products: 104 us -> 24.2 us
  blocking collectives: 57.4 us -> 0 us
  other arithmetic: 44.6 us -> 24.1 us
    pallas_call x0 -> x4, Pallas kernels: none -> 287 us  [the longest x1 139 us: gather_rows(): pl.pallas_call(functools.partial(gather_kernel, chips // 2, cores), out_s...]
    all_gather x4 -> x2, waiting for transfers between devices: 265 us -> 67.6 us  [the longest x1 67.6 us: local(): cached_all = lax.all_gather(cached_key_value, 'ctx', axis=1, tiled=True)]
    dot_general x5 -> x2, matrix products: 95.4 us -> 16 us  [the longest x1 9.24 us: local(): jnp.dot(outputs, out_weight, preferred_element_type=jnp.float32)]
    all_to_all x1 -> x0, blocking collectives: 52.2 us -> none  [local(): lax.all_to_all(product.astype(jnp.bfloat16), 'ctx', split_axis=0, concat_...]
    reduce_sum x3 -> x2, other arithmetic: 37.7 us -> 4.65 us  [the longest x1 3.55 us: local(): head_summed = jnp.sum(parts.astype(jnp.float32), axis=0)]
    reduce_scatter x1 -> x0, waiting for transfers between devices: 33 us -> none  [local(): lax.psum_scatter(partial_sum.astype(jnp.bfloat16), 'head', scatter_dimens...]
    ppermute x0 -> x3, waiting for transfers between devices: none -> 21.7 us  [exchange(): return lax.ppermute(x, axis_name, [(i, i ^ 1) for i in range(size)])]
    slice x4 -> x0, local copies, waits for them, and re-layouts: 11.8 us -> none  [the longest x2 10.1 us: local(): shard_piece[0]]
  transfers between devices with their start and end apart: 5 -> 5, of which waited for: 5 -> 2; matrix products, arithmetic and copies ran while one was open for 5% -> 4% of each run, Pallas kernels for 0% -> 49%
where the time goes in v1:
time: 463 us; the launch traced here: 462 us
  Pallas kernels  287 us (62%)
  waiting for transfers between devices  90 us (19%)
  matrix products  24.2 us (5%)
  other arithmetic  24.1 us (5%)
  local copies, waits for them, and re-layouts  19.6 us (4%)
  between operations  15.1 us (3%)
    pallas_call x1, Pallas kernels, gather_rows(): pl.pallas_call(functools.partial(gather_kernel, chips // 2, cores), out_s...  139 us
    pallas_call x2, Pallas kernels, attend(): pl.pallas_call(functools.partial(attend_kernel, group, last, last), out_s...  88.5 us
    all_gather x1, waiting for transfers between devices, local(): cached_all = lax.all_gather(cached_key_value, 'ctx', axis=1, tiled=True)  67.6 us
    pallas_call x1, Pallas kernels, scatter_columns(): pl.pallas_call(functools.partial(scatter_kernel, chips, cores, heads), ou...  59.4 us
    ppermute x3, waiting for transfers between devices, exchange(): return lax.ppermute(x, axis_name, [(i, i ^ 1) for i in range(size)])  21.7 us
    unnamed x30, local copies, waits for them, and re-layouts  12.7 us
    convert_element_type x1, other arithmetic, local(): full_rows = (widened * level * whole_gain).astype(jnp.bfloat16)  11.2 us
  transfers between devices with their start and end apart: 5, of which 2 were waited for; matrix products, arithmetic and copies ran while one was open for 4% of the time, Pallas kernels for 49%

profile of v1, /device:TPU:28, one launch (start us, length us, event | category | flops | bytes accessed | tf_op | source)
XLA Modules:
  0.0 462.5 jit_solution(14691008060970776861)
XLA Ops:
  7.2 0.7 all-gather.5.cloned.1.call-update
  8.0 0.7 convert_element_type.89
  8.6 1.0 slice_convert_fusion
  9.8 0.3 fusion.5
  10.1 0.3 subtract_convert_fusion.2
  10.4 0.2 pad_maximum_fusion.5
  10.7 0.7 pad_maximum_fusion.3
  11.5 0.2 convert_bitcast_fusion
  11.7 0.4 copy.30
  12.1 0.8 subtract_convert_fusion
  12.9 0.6 pad_maximum_fusion.2
  13.5 0.5 copy.36
  14.0 0.2 copy-done.8
  14.1 1.4 copy.21
  15.5 67.6 %all-gather.5.cloned.1.call-done.k_ref.v_ref = bf16[2,4096,512]{2,1,0:T(8,128)(2,1)} async-done(((bf16[2,256,512]{2,1,0:T(8,128)(2,1)}), bf16[2,4096,512]{2,1,0:T(8,128)(2,1)}) %all-gather.5.cloned.1.call-update) | async-done | bytes 8388624 | tf_op jit(solution)/shard_map/all_gather | solution.py:394
  83.1 58.1 %shard_map.122 = (f32[4,1024,128]{2,1,0:T(8,128)S(1)}, f32[4,1024,128]{2,1,0:T(8,128)S(1)}, f32[4,1024,128]{2,1,0:T(8,128)S(1)}) custom-call(s32[1]{0:T(128)} %bitcast.row_ref, bf16[128,4096]{1,0:T(8,128)(2,1)S(1)} %bitcast.38, bf16[2,4096,512]{2,1,0:T(8,128)(2,1)} %all-gather.5.cloned.1.call-done.k_ref.v_ref, ...), custom_call_target="tpu_custom_call" | custom-call | flops 17179869184 | bytes 10485760 | tf_op jit(solution)/shard_map/pallas_call | solution.py:143
  141.3 1.3 copy-done.2
  142.6 1.3 copy-done.4
  143.9 2.2 copy-done.1
  146.1 1.6 copy-done.3
  147.7 1.6 copy-done.5
  149.3 30.3 %shard_map.123 = bf16[128,4096]{1,0:T(8,128)(2,1)S(1)} custom-call(s32[1]{0:T(128)} %bitcast.row_ref, bf16[128,4096]{1,0:T(8,128)(2,1)S(1)} %bitcast.39, bf16[2,2048,512]{2,1,0:T(8,128)(2,1)S(1)} %copy-done.1, bf16[2,2048,512]{2,1,0:T(8,128)(2,1)S(1)} %copy-done.1, f32[4,1024,128]{2,1,0:T(8,128)S(1)} %get-tuple-element.5.rest_0_, ...), custom_call_target="tpu_custom_call" | custom-call | flops 8589934592 | bytes 6291456 | tf_op jit(solution)/shard_map/pallas_call | solution.py:143
  179.6 1.0 copy-done
  180.6 139.3 %shard_map.124 = bf16[8,2,64,4096]{3,2,1,0:T(8,128)(2,1)} custom-call(bf16[2,64,4096]{2,1,0:T(8,128)(2,1)} %bitcast.37), custom_call_target="tpu_custom_call" | custom-call | tf_op jit(solution)/shard_map/pallas_call | solution.py:330
  319.9 9.2 %convolution_convert_fusion.1 = bf16[1024,512]{0,1:T(8,128)(2,1)S(1)} fusion(bf16[1024,4096]{1,0:T(8,128)(2,1)} %bitcast.41, bf16[4096,512]{1,0:T(8,128)(2,1)} %param.16), kind=kOutput, calls=%fused_computation.15 | convolution fusion | flops 4295491584 | bytes 13631488 | tf_op jit(solution)/shard_map/dot_general | solution.py:399
  329.2 6.7 %broadcast_select_fusion.3 = (bf16[1024,512]{0,1:T(8,128)(2,1)S(1)}, bf16[1024,512]{0,1:T(8,128)(2,1)S(1)}) fusion(bf16[1024,512]{0,1:T(8,128)(2,1)S(1)} %convolution_convert_fusion.1, pred[]{:T(512)S(6)} %eq.34, bf16[1024,4096]{1,0:T(8,128)(2,1)S(1)} %bitcast.42, bf16[4096,512]{1,0:T(8,128)(2,1)} %collective-permute-done), kind=kOutput, calls=%fused_computation.22 | convolution fusion | flops 4296540160 | bytes 15728641 | tf_op jit(solution)/shard_map/dot_general | solution.py:400
  335.9 0.2 pad_maximum_fusion
  336.1 2.6 copy.22
  338.7 59.4 %shard_map.125 = bf16[8,128,1024]{2,1,0:T(8,128)(2,1)} custom-call(bf16[8,128,1024]{2,1,0:T(8,128)(2,1)} %bitcast.43), custom_call_target="tpu_custom_call" | custom-call | tf_op jit(solution)/shard_map/pallas_call | solution.py:236
  398.0 3.6 convert_reduce_fusion
  401.6 1.9 copy.23
  403.5 1.7 fusion.3
  405.3 2.0 collective-permute-start.2
  408.0 21.7 %collective-permute-done.2 = f32[4096]{0:T(1024)S(1)} collective-permute-done((f32[4096]{0:T(1024)S(1)}, f32[4096]{0:T(1024)S(1)}, u32[]{:S(2)}, u32[]{:S(2)}) %collective-permute-start.2) | collective-permute-done | bytes 16416 | tf_op jit(solution)/shard_map/ppermute | solution.py:346
  429.7 1.3 copy.27
  431.1 1.1 fusion
  432.2 11.2 %fusion.2 = bf16[128,8192]{0,1:T(8,128)(2,1)S(1)} fusion(f32[8192]{0:T(1024)S(1)} %pad_maximum_fusion.6, f32[128]{0:T(128)S(1)} %add_rsqrt_fusion, bf16[128,4096]{0,1:T(8,128)(2,1)S(1)} %get-tuple-element.13, bf16[128,4096]{0,1:T(8,128)(2,1)S(1)} %get-tuple-element.12), kind=kLoop, calls=%fused_computation.5 | loop fusion | flops 7340032 | bytes 4227584 | tf_op jit(solution)/shard_map/convert_element_type | solution.py:422
  443.4 8.3 %convolution_add_fusion = f32[128,1024]{1,0:T(8,128)S(1)} fusion(bf16[128,8192]{0,1:T(8,128)(2,1)S(1)} %fusion.2, bf16[8192,1024]{1,0:T(8,128)(2,1)} %param.18, f32[1024]{0:T(1024)S(1)} %copy-done.10), kind=kOutput, calls=%fused_computation.16 | convolution fusion | flops 2147614720 | bytes 19402752 | tf_op jit(solution)/shard_map/dot_general | solution.py:425
  451.7 0.4 reshape.250
  452.1 0.2 slice.59
  452.3 0.3 slice.62
  452.6 0.3 subtract_convert_fusion.1
  453.0 0.2 maximum_bitcast_fusion
  453.2 0.2 pad_maximum_fusion.4
  453.4 0.4 copy.26
  453.8 0.2 convert_element_type.102
  453.9 0.9 gather_fusion
  454.8 0.8 select_select_fusion
  (39 shorter events, 0.7 us)
Async XLA Ops:
  7.2 4.3 copy-start.7
  7.2 75.9 %all-gather.5.cloned.1.call-start = ((), (), s32[]{:S(2)}) async-start(), calls=%async_computation.1 | async-start | bytes 8912896 | tf_op jit(solution)/shard_map/all_gather | solution.py:394
  7.9 136.0 %all-gather.3.cloned.1.call-start = ((), (), s32[]{:S(2)}) async-start(), calls=%async_computation | async-start | bytes 4456448 | tf_op jit(solution)/shard_map/all_gather | solution.py:395
  11.4 317.7 %collective-permute-start = (bf16[4096,512]{1,0:T(8,128)(2,1)}, bf16[4096,512]{1,0:T(8,128)(2,1)}, u32[]{:S(2)}, u32[]{:S(2)}) collective-permute-start(bf16[4096,512]{1,0:T(8,128)(2,1)} %param.16), channel_id=1, source_target_pairs={{0,2},{2,0},{4,6},{6,4},{8,10},{10,8},{12,14},{14,12},{16,18},{18,... | collective-permute-start | bytes 12582920 | tf_op jit(solution)/shard_map/ppermute | solution.py:346
  12.9 1.2 copy-start.8
  141.3 1.3 copy-start.2
  142.6 1.3 copy-start.4
  143.9 2.2 copy-start.1
  146.1 1.6 copy-start.3
  147.7 1.6 copy-start.5
  179.6 1.0 copy-start
  319.9 9.3 %copy-start.6 = (bf16[8,2,64,4096]{3,2,1,0:T(8,128)(2,1)S(1)}, bf16[8,2,64,4096]{3,2,1,0:T(8,128)(2,1)}, u32[]{:S(2)}) copy-start(bf16[8,2,64,4096]{3,2,1,0:T(8,128)(2,1)} %shard_map.124) | copy-start | bytes 25165828
  403.5 1.8 copy-start.9
  403.5 4.4 copy-start.11
  405.2 25.8 %collective-permute-start.1 = (bf16[128,4096]{0,1:T(8,128)(2,1)S(1)}, bf16[128,4096]{0,1:T(8,128)(2,1)S(1)}, u32[]{:S(2)}, u32[]{:S(2)}) collective-permute-start(bf16[128,4096]{0,1:T(8,128)(2,1)S(1)} %fusion.3), channel_id=1, source_target_pairs={{0,1},{1,0},{2,3},{3,2},{4,5},{5,4},{6,7},{7,6},{8,9},{9,8},{10,11... | collective-permute-start | bytes 3145736 | tf_op jit(solution)/shard_map/ppermute | solution.py:346
  405.3 24.4 %collective-permute-start.2 = (f32[4096]{0:T(1024)S(1)}, f32[4096]{0:T(1024)S(1)}, u32[]{:S(2)}, u32[]{:S(2)}) collective-permute-start(f32[4096]{0:T(1024)S(1)} %copy-done.9), channel_id=1, source_target_pairs={{0,1},{1,0},{2,3},{3,2},{4,5},{5,4},{6,7},{7,6},{8,9},{9,8},{10,11... | collective-permute-start | bytes 49160 | tf_op jit(solution)/shard_map/ppermute | solution.py:346
  432.2 11.2 %copy-start.10 = (f32[1024]{0:T(1024)S(1)}, f32[1024]{0:T(1024)}, u32[]{:S(2)}) copy-start(f32[1024]{0:T(1024)} %param.19) | copy-start | bytes 12292
Sparse Core Ops, SparseCore 0:
  10.2 72.8 all-gather.4
  85.9 48.9 all-gather.2
